TPU v7x, 32 devices: a whole 2x2x4 slice. The times are simulated.
32 devices in a mesh: outer: 4 (over y, core), inner: 8 (over z, x).
Axes of the slice: x: 2, y: 2, z: 4, core: 2. Of those that a mesh axis runs over, the one named last changes fastest.
Arguments:
- amplitudes: float32 [2, 8388608], P(None, ('outer', 'inner')), may hold values from -200 to 200
Outputs:
- transformed: float32 [2, 8388608], P(None, ('outer', 'inner'))
- checks: float32 [3], replicated
All inputs are finite; a program needn't handle non-finite values.
Results may differ from a plain program's by a relative error of at most 0.00007.
Values sent between devices are 32-bit elements; how exact they have to be, the bound alone decides.
No kernel may reach another device: no remote copies, remote signals or barrier semaphores. Data moves between devices by JAX's collectives and lax.ppermute only.
A program may use at most 64 MiB of HBM per device.

v0:
```python
import math

import jax
import jax.numpy as jnp
import ml_dtypes
import numpy as np
from jax import lax
from jax.experimental import pallas as pl
from jax.experimental.pallas import tpu as pltpu
from jax.sharding import PartitionSpec as P


WINDOW = 9
LANES = 128
RADIX = 2**WINDOW // LANES
AXES = ("outer", "inner")
VMEM_LIMIT = 16 * 2**20
SUB = 16
LEADS = 2
START_ORDER = (7, 0, 2, 3, 4, 5, 8, 9, 10, 11, 12, 13, 1, 14, 6)


def flip(value, count):
    result = 0
    for bit_pos in range(count):
        result |= (value >> bit_pos & 1) << count - 1 - bit_pos
    return result


def split_halves(table):
    high = table.astype(ml_dtypes.bfloat16)
    low = (table - high.astype(np.float64)).astype(ml_dtypes.bfloat16)
    return high, low


def transform_tables(n_devices):
    columns = 2**WINDOW
    freq = np.arange(LANES) * RADIX
    sample = np.arange(LANES)
    tables = []
    for residue in range(RADIX):
        angles = (freq + residue)[:, None] * sample[None, :] % columns * (2 * np.pi / columns)
        cosine = np.cos(angles) / math.sqrt(columns)
        sine = np.sin(angles) / math.sqrt(columns)
        rows = np.stack([np.concatenate([cosine, -sine], 1), np.concatenate([sine, cosine], 1)], 1)
        tables.append(rows.reshape(n_devices // 2, 2, 8, 2 * LANES))
    high, low = split_halves(np.stack(tables))
    both = np.concatenate([high, low], 0).transpose(1, 0, 2, 3, 4)
    both = np.stack([both, both[:, :, ::-1]])
    return both.reshape(2, n_devices // 2, 2 * RADIX, 16, 2 * LANES)


def phase_tables(chunks, n_devices, angle_scale):
    turn = np.array([flip(row, LANES.bit_length() - 1) for row in range(LANES)])
    angles = turn * float(chunks * n_devices) * angle_scale
    table = np.zeros((2, LANES, LANES))
    table[0, :, 1] = np.cos(angles)
    table[1, :, 1] = np.sin(angles)
    return table.astype(np.float32)


def plan(n_outer, n_inner):
    core_bit, far_bit = n_inner, n_inner // 2
    chip_masks = [mask for mask in range(1, n_outer * n_inner) if not mask & core_bit]
    blocks = sorted(chip_masks, key=lambda mask: (not mask & far_bit, mask.bit_count()))
    ordered = [blocks[place] for place in START_ORDER if place < len(blocks)]
    leads, rest = ordered[:LEADS], ordered[LEADS:]
    far = [mask for mask in rest if mask & far_bit]
    near = [mask for mask in rest if not mask & far_bit]
    return leads, far, near, [(far + near).index(mask) for mask in rest]


def fits(amp_dev, n_outer, n_inner):
    n_devices = n_outer * n_inner
    chunks = amp_dev // 2**WINDOW // LANES
    same_tile = 2**WINDOW // n_devices // RADIX * 2 == 8
    return chunks * n_devices == LANES and same_tile and n_inner > 1 and n_outer > 1


def halves(values):
    high = values.astype(jnp.bfloat16)
    low = (values - high.astype(jnp.float32)).astype(jnp.bfloat16)
    return high, low


def dot_rows(left, right):
    return lax.dot_general(
        left, right, (((1,), (1,)), ((), ())), preferred_element_type=jnp.float32
    )


def transform_kernel(info, targets, tiles, x_hbm, table_hbm, phase_hbm, *refs):
    n_devices, chunks, angle_scale, device_id = info()
    outs, (x_ref, table_ref, phase_ref, high_ref, low_ref, sems) = refs[:-6], refs[-6:]
    chunk_rows = RADIX * 8
    x_rows = x_ref.shape[0] // chunks
    dev_bits = n_devices.bit_length() - 1
    chunk_bits = chunks.bit_length() - 1

    def load(source, target, index):
        return pltpu.make_async_copy(source, target, sems.at[index])

    loads = []
    for chunk in range(chunks):
        rows = pl.ds(chunk * x_rows, x_rows)
        loads.append(load(x_hbm.at[rows], x_ref.at[rows], chunk))
    phase_load = load(phase_hbm, phase_ref, chunks)
    table_loads = [
        load(
            table_hbm.at[device_id & 1, (device_id >> 1) ^ block],
            table_ref.at[block],
            chunks + 1 + block,
        )
        for block in range(n_devices // 2)
    ]
    for copy in loads[:1] + [phase_load] + loads[1:] + table_loads:
        copy.start()

    base = jnp.int32(0)
    for bit in range(dev_bits):
        base += (device_id >> bit & 1) << (dev_bits - 1 - bit)
    square_sum = real_sum = imag_sum = jnp.zeros((8, LANES), jnp.float32)
    fold = lambda value: value.reshape(SUB // 8, 8, LANES).sum(0)
    for half in range(chunks // 2):
        for chunk in (2 * half, 2 * half + 1):
            loads[chunk].wait()
            if chunk == 0:
                phase_load.wait()
            turn_re = turn_im = jnp.zeros((8, LANES), jnp.float32)
            for sub in range(LANES // SUB):
                start = chunk * x_rows + sub * SUB * 2 * RADIX
                parts = [
                    [x_ref[pl.ds(start + 2 * j + s, SUB, stride=2 * RADIX), :] for s in range(2)]
                    for j in range(RADIX)
                ]
                square_sum += fold(sum(p * p for pair in parts for p in pair))
                cosine = phase_ref[0, sub * SUB : (sub + 1) * SUB]
                sine = phase_ref[1, sub * SUB : (sub + 1) * SUB]
                first_re, first_im = parts[0]
                turn_re += fold(first_re * cosine + first_im * sine)
                turn_im += fold(first_im * cosine - first_re * sine)
                (r0, i0), (r1, i1), (r2, i2), (r3, i3) = parts
                ar, ai, br, bi = r0 + r2, i0 + i2, r0 - r2, i0 - i2
                cr, ci, dr, di = r1 + r3, i1 + i3, r1 - r3, i1 - i3
                folded = [
                    (ar + cr, ai + ci),
                    (br - di, bi + dr),
                    (ar - cr, ai - ci),
                    (br + di, bi - dr),
                ]
                row = (chunk % 2) * LANES + sub * SUB
                for residue in range(RADIX):
                    for part in range(2):
                        high, low = halves(folded[residue][part])
                        where = (half, residue, pl.ds(row, SUB), pl.ds(part * LANES, LANES))
                        high_ref[where] = high
                        low_ref[where] = low
            angle = flip(chunk, chunk_bits) * n_devices * angle_scale
            cosine, sine = math.cos(angle), math.sin(angle)
            real_sum += turn_re * cosine + turn_im * sine
            imag_sum += turn_im * cosine - turn_re * sine
    for copy in table_loads:
        copy.wait()
    for half in range(chunks // 2):
        for residue in range(RADIX):
            table_high = table_ref[:, residue].reshape(2 * LANES, 2 * LANES)
            table_low = table_ref[:, RADIX + residue].reshape(2 * LANES, 2 * LANES)
            high, low = high_ref[half, residue], low_ref[half, residue]
            values = dot_rows(table_high, high) + dot_rows(table_high, low)
            values += dot_rows(table_low, high)
            for mask, out, row in targets:
                for part in range(2):
                    rows = pl.ds(row + (2 * half + part) * chunk_rows + residue * 8, 8)
                    outs[out][rows, :] = values[
                        8 * mask : 8 * mask + 8, part * LANES : (part + 1) * LANES
                    ]

    theta = jnp.full((8, LANES), base, jnp.int32).astype(jnp.float32) * angle_scale
    theta_sq = theta * theta
    cosine = 1.0 - theta_sq * (0.5 - theta_sq * (1.0 / 24.0))
    sine = theta * (1.0 - theta_sq * (1.0 / 6.0 - theta_sq * (1.0 / 120.0)))
    turned = (square_sum, real_sum * cosine + imag_sum * sine, imag_sum * cosine - real_sum * sine)
    sums = [value.sum(0, keepdims=True) for value in turned]
    tile = jnp.concatenate(sums + [jnp.zeros((5, LANES), jnp.float32)], 0)
    for out, row in tiles:
        outs[out][pl.ds(row, 8), :] = tile


def join_kernel(rows, first, stamps, n_join, swapped_ref, *refs):
    refs = (swapped_ref,) + refs
    outs = refs[len(refs) - n_join :]
    tile = None
    for operand, row in stamps:
        value = refs[operand][pl.ds(row, 8), :]
        tile = value if tile is None else tile + value
    for index, out in enumerate(outs):
        out[pl.ds(rows, rows), :] = swapped_ref[pl.ds((first + index) * rows, rows), :]
        if tile is not None:
            out[pl.ds(2 * rows, 8), :] = tile


def keep(info, sources, ins, held):
    n_devices, chunks, _, _, device_id = info()
    dev_bits = n_devices.bit_length() - 1
    slot_rows = held.shape[0] // n_devices
    turned_id = jnp.int32(0)
    for bit in range(dev_bits):
        turned_id += (device_id >> bit & 1) << (dev_bits - 1 - bit)
    rows = chunks * RADIX * 8
    for mask, array, offset in sources:
        slot = turned_id ^ flip(mask, dev_bits)
        target = pl.ds(pl.multiple_of(slot * slot_rows, 8), rows)
        held[target, :] = ins[array][pl.ds(offset, rows), :]


def stash_kernel(info, sources, tiles, *refs):
    ins, (held, sum_ref) = refs[:-2], refs[-2:]
    keep(info, sources, ins, held)
    tile = jnp.zeros((8, LANES), jnp.float32)
    for array, offset in tiles:
        tile = tile + ins[array][pl.ds(offset, 8), :]
    sum_ref[...] = tile


def place_kernel(info, sources, order_ref, held_ref, sum_ref, *refs):
    n_devices, chunks, groups, total_len, _ = info()
    ins = refs[:-5]
    out_hbm, checks_ref, held, out_ref, sems = refs[-5:]
    chunk_bits = chunks.bit_length() - 1
    slot_rows = held.shape[0] // n_devices
    keep(info, sources, ins, held)
    tile = sum_ref[...]
    sums = tile.sum(1, keepdims=True)
    mean_square = jnp.broadcast_to(sums[0:1], (8, LANES)) * (1.0 / total_len)
    shifted = mean_square + 1e-06
    factor = lax.rsqrt(shifted)
    factor = factor * (1.5 - 0.5 * shifted * factor * factor)
    columns = 2**WINDOW
    scaled = factor * math.sqrt(columns / total_len)
    checks_ref[0] = mean_square[0, 0]
    checks_ref[1] = (jnp.broadcast_to(sums[1:2], (8, LANES)) * scaled)[0, 0]
    checks_ref[2] = (jnp.broadcast_to(sums[2:3], (8, LANES)) * scaled)[0, 0]

    factor = jnp.broadcast_to(factor[0:1], (LANES, LANES))
    order = order_ref[...]
    copies = []
    for group in range(groups):
        for residue in range(RADIX):
            for part in range(2):
                pieces = []
                for low in range(chunks):
                    tile_row = (flip(low, chunk_bits) * RADIX + residue) * 8 + 2 * group + part
                    pieces.append(held[pl.ds(tile_row, n_devices, stride=slot_rows), :])
                high, low = halves(jnp.concatenate(pieces, 0))
                turned = dot_rows(order, jnp.concatenate([high, low], 1))
                row = (group * RADIX + residue) * 2 * LANES + part
                out_ref[pl.ds(row, LANES, stride=2), :] = turned * factor
            if residue % 2 == 1:
                size = 4 * LANES
                span = pl.ds(len(copies) * size, size)
                sem = sems.at[len(copies)]
                copies.append(pltpu.make_async_copy(out_ref.at[span], out_hbm.at[span], sem))
                copies[-1].start()
    for copy in copies:
        copy.wait()


def reverse_index(values, count):
    result = jnp.zeros_like(values)
    for bit_pos in range(count):
        result = result | (values >> bit_pos & 1) << count - 1 - bit_pos
    return result


def reversal_table(size, count):
    indices = jnp.arange(size, dtype=jnp.int32)
    return (reverse_index(indices, count)[:, None] == indices[None, :]).astype(jnp.float32)


def check_terms(current, positions, angle_scale):
    angles = positions.astype(jnp.float32) * angle_scale
    cosine = jnp.cos(angles)
    sine = jnp.sin(angles)
    squares = jnp.sum(current * current)
    phase_real = jnp.sum(current[0] * cosine + current[1] * sine)
    phase_imag = jnp.sum(current[1] * cosine - current[0] * sine)
    return (squares, phase_real, phase_imag)


def general_device(amplitudes):
    amp_dev = amplitudes.shape[1]
    n_outer = lax.axis_size("outer")
    n_inner = lax.axis_size("inner")
    outer_bits = n_outer.bit_length() - 1
    inner_bits = n_inner.bit_length() - 1
    global_bits = outer_bits + inner_bits
    local_bits = amp_dev.bit_length() - 1
    n_devices = n_outer * n_inner
    high_count = amp_dev // n_devices
    total_len = amp_dev * n_devices
    columns = 2**WINDOW
    rows_count = amp_dev // columns
    column_ids = jnp.arange(columns, dtype=jnp.int32)
    reversed_ids = reverse_index(column_ids, WINDOW)
    products = column_ids[:, None] * reversed_ids[None, :] % columns
    angles = products.astype(jnp.float32) * (2.0 * math.pi / columns)
    real_part = jnp.cos(angles) / math.sqrt(columns)
    imag_part = jnp.sin(angles) / math.sqrt(columns)
    table = jnp.concatenate(
        [jnp.concatenate([real_part, imag_part], 1), jnp.concatenate([-imag_part, real_part], 1)], 0
    )
    stacked = jnp.concatenate(
        [amplitudes[0].reshape(rows_count, columns), amplitudes[1].reshape(rows_count, columns)], 1
    )
    result = jnp.dot(
        stacked, table, precision=lax.Precision.HIGHEST, preferred_element_type=jnp.float32
    )
    windowed = jnp.stack([result[:, :columns].reshape(-1), result[:, columns:].reshape(-1)])
    device_id = lax.axis_index("outer") * n_inner + lax.axis_index("inner")
    angle_scale = 2.0 * math.pi / total_len
    local_ids = jnp.arange(amp_dev, dtype=jnp.int32)
    positions = reverse_index(device_id * amp_dev + local_ids, local_bits + global_bits)
    totals = lax.psum(check_terms(windowed, positions, angle_scale), ("outer", "inner"))
    device_table = reversal_table(n_devices, global_bits)
    high_table = reversal_table(high_count, local_bits - global_bits)
    grid = windowed.reshape(2, high_count, n_devices)
    ordered = jnp.einsum("pm,shm->sph", device_table, grid, precision=lax.Precision.HIGHEST)
    blocks = ordered.reshape(2, n_outer, n_inner, high_count)
    blocks = lax.all_to_all(
        lax.all_to_all(blocks, "outer", split_axis=1, concat_axis=1, tiled=True),
        "inner",
        split_axis=2,
        concat_axis=2,
        tiled=True,
    )
    received = blocks.reshape(2, n_devices, high_count)
    turned_high = jnp.einsum("qh,sdh->sdq", high_table, received, precision=lax.Precision.HIGHEST)
    placed = jnp.einsum("ed,sdq->sqe", device_table, turned_high, precision=lax.Precision.HIGHEST)
    reversed_field = placed.reshape(2, amp_dev)
    mean_square = totals[0] / total_len
    factor = lax.rsqrt(mean_square + 1e-06)
    scaled = factor / math.sqrt(total_len)
    checks = jnp.stack([mean_square, totals[1] * scaled, totals[2] * scaled])
    return (reversed_field * factor, checks)


def per_device(amplitudes):
    amp_dev = amplitudes.shape[1]
    n_devices = lax.axis_size("outer") * lax.axis_size("inner")
    n_inner = lax.axis_size("inner")
    total_len = amp_dev * n_devices
    columns = 2**WINDOW
    rows_count = amp_dev // columns
    chunks = rows_count // LANES
    groups = columns // n_devices // RADIX
    if not fits(amp_dev, lax.axis_size("outer"), n_inner):
        return general_device(amplitudes)
    vectors = 2 * amp_dev // LANES
    slot_rows = chunks * RADIX * 8 + 8
    x = amplitudes.reshape(2, vectors // 2, LANES).transpose(1, 0, 2).reshape(vectors, LANES)
    angle_scale = 2.0 * math.pi / total_len
    table = transform_tables(n_devices)
    phase = phase_tables(chunks, n_devices, angle_scale)
    turn = np.array([flip(lane, LANES.bit_length() - 1) for lane in range(LANES)])
    order = (turn[:, None] == np.arange(LANES)[None, :]).astype(np.float32)
    order = np.concatenate([order, order], 1).astype(ml_dtypes.bfloat16)

    rows = chunks * RADIX * 8
    core_bit = n_inner
    direct, far, near, _ = plan(lax.axis_size("outer"), n_inner)
    pairs = far + near
    n_pairs = len(pairs)
    n_far = len(far)

    def info():
        device_id = lax.axis_index("outer") * n_inner + lax.axis_index("inner")
        return n_devices, chunks, angle_scale, device_id

    def place_info():
        return n_devices, chunks, groups, total_len, info()[3]

    def exchange(values, mask):
        pairs_of = [(source, source ^ mask) for source in range(n_devices)]
        return lax.ppermute(values, AXES, pairs_of)

    singles = [mask ^ core for mask in direct for core in (0, core_bit)]
    swap_rows = (n_pairs + 1) * rows
    pair_rows = [2 * rows] * len(far) + [2 * rows + 8] * len(near)
    single_rows = [rows + 8] * 2 + [rows] * (len(singles) - 2)
    all_rows = pair_rows + [rows + 8, swap_rows + 8] + single_rows
    stay, swap = n_pairs, n_pairs + 1
    targets = [(mask, index, 0) for index, mask in enumerate(pairs)] + [(0, stay, 0)]
    targets += [(mask ^ core_bit, swap, index * rows) for index, mask in enumerate(pairs + [0])]
    targets += [(mask, swap + 1 + index, 0) for index, mask in enumerate(singles)]
    tiles = [(stay, rows), (swap, swap_rows), (swap + 1, rows), (swap + 2, rows)]
    constrain = lambda value: pltpu.with_memory_space_constraint(value, pltpu.HBM)
    shaped = lambda count: jax.ShapeDtypeStruct((count, LANES), jnp.float32)
    hbm = pl.BlockSpec(memory_space=pltpu.HBM)
    vmem = pl.BlockSpec(memory_space=pltpu.VMEM)
    sent = pl.pallas_call(
        lambda *refs: transform_kernel(info, targets, tiles, *refs),
        in_specs=[hbm] * 3,
        out_specs=[vmem] * len(all_rows),
        out_shape=[shaped(count) for count in all_rows],
        scratch_shapes=[
            pltpu.VMEM((vectors, LANES), jnp.float32),
            pltpu.VMEM(table.shape[1:], jnp.bfloat16),
            pltpu.VMEM(phase.shape, jnp.float32),
            pltpu.VMEM((chunks // 2, RADIX, 2 * LANES, 2 * LANES), jnp.bfloat16),
            pltpu.VMEM((chunks // 2, RADIX, 2 * LANES, 2 * LANES), jnp.bfloat16),
            pltpu.SemaphoreType.DMA((chunks + 1 + n_devices // 2,)),
        ],
        compiler_params=pltpu.CompilerParams(vmem_limit_bytes=VMEM_LIMIT),
        name="transform",
    )(constrain(x), constrain(jnp.asarray(table)), constrain(jnp.asarray(phase)))
    swapped = exchange(sent[swap], core_bit)
    arrived_singles = []
    for index, mask in enumerate(singles):
        arrived_singles.append(exchange(sent[swap + 1 + index], mask))

    def join(first, count, extra, stamps):
        n_extra = len(extra)
        return pl.pallas_call(
            lambda *refs: join_kernel(rows, first, stamps, count, *refs),
            in_specs=[vmem] * (1 + n_extra + count),
            out_specs=[vmem] * count,
            out_shape=[shaped(size) for size in pair_rows[first : first + count]],
            input_output_aliases={1 + n_extra + i: i for i in range(count)},
            compiler_params=pltpu.CompilerParams(vmem_limit_bytes=VMEM_LIMIT),
            name="join",
        )(swapped, *extra, *sent[first : first + count])

    joined = join(0, len(far), [], [])
    stamps = [(0, swap_rows), (1, rows), (2, rows), (3, rows)]
    joined += join(len(far), len(near), [sent[stay]] + arrived_singles[:2], stamps)
    arrived_pairs = []
    for index, mask in enumerate(pairs):
        arrived_pairs.append(exchange(joined[index], mask))
    arrivals = arrived_pairs + [sent[stay], swapped] + arrived_singles
    sources = []
    for index, mask in enumerate(pairs):
        sources += [(mask, index, 0), (mask ^ core_bit, index, rows)]
    sources += [(0, stay, 0), (core_bit, swap, n_pairs * rows)]
    sources += [(mask, swap + 1 + index, 0) for index, mask in enumerate(singles)]
    sums = tiles + [(len(far) + index, 2 * rows) for index in range(len(near))]
    params = pltpu.CompilerParams(vmem_limit_bytes=VMEM_LIMIT)
    held_rows = n_devices * slot_rows
    n_late = 2
    late = range(n_far - n_late, n_far)
    late_sources = [(mask, index - late[0], row) for mask, index, row in sources if index in late]
    early_sources = [source for source in sources if source[1] not in late]
    early = [index for index in range(len(arrivals)) if index not in late]
    renamed = lambda index: early.index(index)
    early_sources = [(mask, renamed(index), row) for mask, index, row in early_sources]
    sums = [(renamed(index), row) for index, row in sums]
    held, total = pl.pallas_call(
        lambda *refs: stash_kernel(place_info, early_sources, sums, *refs),
        in_specs=[vmem] * len(early),
        out_specs=[vmem, vmem],
        out_shape=[shaped(held_rows), shaped(8)],
        compiler_params=params,
        name="stash",
    )(*[arrivals[index] for index in early])
    placed, checks, _ = pl.pallas_call(
        lambda *refs: place_kernel(place_info, late_sources, *refs),
        in_specs=[vmem] * (3 + n_late),
        out_specs=[hbm, pl.BlockSpec(memory_space=pltpu.SMEM), vmem],
        out_shape=[
            jax.ShapeDtypeStruct((vectors, LANES), jnp.float32),
            jax.ShapeDtypeStruct((3,), jnp.float32),
            shaped(held_rows),
        ],
        input_output_aliases={1: 2},
        scratch_shapes=[
            pltpu.VMEM((vectors, LANES), jnp.float32),
            pltpu.SemaphoreType.DMA((2 * groups,)),
        ],
        compiler_params=params,
        name="place",
    )(jnp.asarray(order), held, total, *[arrivals[index] for index in late])
    placed = placed.reshape(vectors // 2, 2, LANES).transpose(1, 0, 2).reshape(2, amp_dev)
    return placed, checks


def solution(mesh):
    return jax.shard_map(
        per_device,
        mesh=mesh,
        in_specs=(P(None, ("outer", "inner")),),
        out_specs=(P(None, ("outer", "inner")), P()),
        check_vma=False,
    )
```

profile of v0, /device:TPU:0, one launch (start us, length us, event | category | flops | bytes accessed | tf_op | source)
XLA Modules:
  0.0 70.3 jit_solution(7157998491018698906)
XLA Ops:
  0.6 3.1 %transform.1 = (f32[256,128]{1,0:T(8,128)S(1)}, f32[256,128]{1,0:T(8,128)S(1)}, f32[256,128]{1,0:T(8,128)S(1)}, f32[256,128]{1,0:T(8,128)S(1)}, f32[256,128]{1,0...) custom-call(f32[4096,128]{1,0:T(8,128)} %bitcast.10, ...), custom_call_target="tpu_custom_call" | custom-call | tf_op jit(solution)/shard_map/transform/pallas_call | solution.py:400
  3.7 0.6 collective-permute-start
  4.2 6.5 %collective-permute-start.5 = (f32[136,128]{1,0:T(8,128)S(1)}, f32[136,128]{1,0:T(8,128)S(1)}, u32[]{:S(2)}, u32[]{:S(2)}) collective-permute-start(f32[136,128]{1,0:T(8,128)S(1)} %get-tuple-element.50), channel_id=1, source_target_pairs={{0,23},{1,22},{2,21},{3,20},{4,19},{5,18},{6,17},{7,16},{8,31},{9,... | collective-permute-start | bytes 208904 | tf_op jit(solution)/shard_map/ppermute | solution.py:384
  10.8 0.0 collective-permute-start.6
  10.8 0.0 collective-permute-done.refs_0_.refs_12_
  10.9 3.5 %collective-permute-start.1 = (f32[256,128]{1,0:T(8,128)S(1)}, f32[256,128]{1,0:T(8,128)S(1)}, u32[]{:S(2)}, u32[]{:S(2)}) collective-permute-start(f32[256,128]{1,0:T(8,128)S(1)} %get-tuple-element.45), channel_id=1, source_target_pairs={{0,6},{1,7},{2,4},{3,5},{4,2},{5,3},{6,0},{7,1},{8,14},{9,15},{10,... | collective-permute-start | bytes 393224 | tf_op jit(solution)/shard_map/ppermute | solution.py:384
  14.4 2.0 %collective-permute-start.3 = (f32[256,128]{1,0:T(8,128)S(1)}, f32[256,128]{1,0:T(8,128)S(1)}, u32[]{:S(2)}, u32[]{:S(2)}) collective-permute-start(f32[256,128]{1,0:T(8,128)S(1)} %get-tuple-element.47), channel_id=1, source_target_pairs={{0,7},{1,6},{2,5},{3,4},{4,3},{5,2},{6,1},{7,0},{8,15},{9,14},{10,... | collective-permute-start | bytes 393224 | tf_op jit(solution)/shard_map/ppermute | solution.py:384
  16.4 2.1 %collective-permute-start.14 = (f32[128,128]{1,0:T(8,128)S(1)}, f32[128,128]{1,0:T(8,128)S(1)}, u32[]{:S(2)}, u32[]{:S(2)}) collective-permute-start(f32[128,128]{1,0:T(8,128)S(1)} %get-tuple-element.66), channel_id=1, source_target_pairs={{0,4},{1,5},{2,6},{3,7},{4,0},{5,1},{6,2},{7,3},{8,12},{9,13},{10,... | collective-permute-start | bytes 196616 | tf_op jit(solution)/shard_map/ppermute | solution.py:384
  18.5 0.1 collective-permute-done.6.refs_3_.refs_14_
  18.6 0.2 collective-permute-start.15
  18.8 20.0 %collective-permute-done.14.refs_15_ = f32[128,128]{1,0:T(8,128)S(1)} collective-permute-done((f32[128,128]{1,0:T(8,128)S(1)}, f32[128,128]{1,0:T(8,128)S(1)}, u32[]{:S(2)}, u32[]{:S(2)}) %collective-permute-start.14) | collective-permute-done | bytes 65568 | tf_op jit(solution)/shard_map/ppermute | solution.py:384
  38.8 0.5 collective-permute-start.7
  39.3 3.7 %collective-permute-start.4 = (f32[256,128]{1,0:T(8,128)S(1)}, f32[256,128]{1,0:T(8,128)S(1)}, u32[]{:S(2)}, u32[]{:S(2)}) collective-permute-start(f32[256,128]{1,0:T(8,128)S(1)} %get-tuple-element.48), channel_id=1, source_target_pairs={{0,21},{1,20},{2,23},{3,22},{4,17},{5,16},{6,19},{7,18},{8,29},{9,... | collective-permute-start | bytes 393224 | tf_op jit(solution)/shard_map/ppermute | solution.py:384
  43.0 1.8 %collective-permute-start.9 = (f32[264,128]{1,0:T(8,128)S(1)}, f32[264,128]{1,0:T(8,128)S(1)}, u32[]{:S(2)}, u32[]{:S(2)}) collective-permute-start(f32[264,128]{1,0:T(8,128)S(1)} %get-tuple-element.61), channel_id=1, source_target_pairs={{0,16},{1,17},{2,18},{3,19},{4,20},{5,21},{6,22},{7,23},{8,24},{9,... | collective-permute-start | bytes 405512 | tf_op jit(solution)/shard_map/ppermute | solution.py:384
  44.8 5.8 %collective-permute-done.4.refs_3_ = f32[256,128]{1,0:T(8,128)S(1)} collective-permute-done((f32[256,128]{1,0:T(8,128)S(1)}, f32[256,128]{1,0:T(8,128)S(1)}, u32[]{:S(2)}, u32[]{:S(2)}) %collective-permute-start.4) | collective-permute-done | bytes 131104 | tf_op jit(solution)/shard_map/ppermute | solution.py:384
  50.6 0.7 collective-permute-start.11
  51.2 2.2 %collective-permute-start.12 = (f32[264,128]{1,0:T(8,128)S(1)}, f32[264,128]{1,0:T(8,128)S(1)}, u32[]{:S(2)}, u32[]{:S(2)}) collective-permute-start(f32[264,128]{1,0:T(8,128)S(1)} %get-tuple-element.64), channel_id=1, source_target_pairs={{0,18},{1,19},{2,16},{3,17},{4,22},{5,23},{6,20},{7,21},{8,26},{9,... | collective-permute-start | bytes 405512 | tf_op jit(solution)/shard_map/ppermute | solution.py:384
  53.4 1.5 %collective-permute-start.13 = (f32[264,128]{1,0:T(8,128)S(1)}, f32[264,128]{1,0:T(8,128)S(1)}, u32[]{:S(2)}, u32[]{:S(2)}) collective-permute-start(f32[264,128]{1,0:T(8,128)S(1)} %get-tuple-element.65), channel_id=1, source_target_pairs={{0,19},{1,18},{2,17},{3,16},{4,23},{5,22},{6,21},{7,20},{8,27},{9,... | collective-permute-start | bytes 405512 | tf_op jit(solution)/shard_map/ppermute | solution.py:384
  54.9 2.0 %collective-permute-start.16 = (f32[256,128]{1,0:T(8,128)S(1)}, f32[256,128]{1,0:T(8,128)S(1)}, u32[]{:S(2)}, u32[]{:S(2)}) collective-permute-start(f32[256,128]{1,0:T(8,128)S(1)} %get-tuple-element.70), channel_id=1, source_target_pairs={{0,5},{1,4},{2,7},{3,6},{4,1},{5,0},{6,3},{7,2},{8,13},{9,12},{10,... | collective-permute-start | bytes 393224 | tf_op jit(solution)/shard_map/ppermute | solution.py:384
  56.9 2.7 %collective-permute-start.17 = (f32[256,128]{1,0:T(8,128)S(1)}, f32[256,128]{1,0:T(8,128)S(1)}, u32[]{:S(2)}, u32[]{:S(2)}) collective-permute-start(f32[256,128]{1,0:T(8,128)S(1)} %get-tuple-element.71), channel_id=1, source_target_pairs={{0,22},{1,23},{2,20},{3,21},{4,18},{5,19},{6,16},{7,17},{8,30},{9,... | collective-permute-start | bytes 393224 | tf_op jit(solution)/shard_map/ppermute | solution.py:384
  59.6 2.4 %collective-permute-done.11.refs_8_ = f32[264,128]{1,0:T(8,128)S(1)} collective-permute-done((f32[264,128]{1,0:T(8,128)S(1)}, f32[264,128]{1,0:T(8,128)S(1)}, u32[]{:S(2)}, u32[]{:S(2)}) %collective-permute-start.11) | collective-permute-done | bytes 135200 | tf_op jit(solution)/shard_map/ppermute | solution.py:384
  62.0 0.1 stash.1
  62.1 6.0 %collective-permute-done.16.refs_3_ = f32[256,128]{1,0:T(8,128)S(1)} collective-permute-done((f32[256,128]{1,0:T(8,128)S(1)}, f32[256,128]{1,0:T(8,128)S(1)}, u32[]{:S(2)}, u32[]{:S(2)}) %collective-permute-start.16) | collective-permute-done | bytes 131104 | tf_op jit(solution)/shard_map/ppermute | solution.py:384
  68.1 2.2 %place.1 = (f32[4096,128]{1,0:T(8,128)}, f32[3]{0:T(128)}, f32[4352,128]{1,0:T(8,128)S(1)}) custom-call(bf16[128,256]{1,0:T(8,128)(2,1)S(1)} %copy-done, f32[4352,128]{1,0:T(8,128)S(1)} %get-tuple-element.68.refs_1_, f32[8,128]{1,0:T(8,128)S(1)} %get-tuple-element.69.refs_2_, ...), custom_call_target="tpu_custom_call", output_to_operand_aliasing={{2}: (1, {})} | custom-call | tf_op jit(solution)/shard_map/place/pallas_call | solution.py:464
  (19 shorter events, 0.1 us)
Async XLA Ops:
  3.7 7.1 %collective-permute-start = (f32[1800,128]{1,0:T(8,128)S(1)}, f32[1800,128]{1,0:T(8,128)S(1)}, u32[]{:S(2)}, u32[]{:S(2)}) collective-permute-start(f32[1800,128]{1,0:T(8,128)S(1)} %get-tuple-element.38), channel_id=1, source_target_pairs={{0,8},{1,9},{2,10},{3,11},{4,12},{5,13},{6,14},{7,15},{8,0},{9,1},... | collective-permute-start | bytes 2764808 | tf_op jit(solution)/shard_map/ppermute | solution.py:384
  4.2 12.1 %collective-permute-start.5 = (f32[136,128]{1,0:T(8,128)S(1)}, f32[136,128]{1,0:T(8,128)S(1)}, u32[]{:S(2)}, u32[]{:S(2)}) collective-permute-start(f32[136,128]{1,0:T(8,128)S(1)} %get-tuple-element.50), channel_id=1, source_target_pairs={{0,23},{1,22},{2,21},{3,20},{4,19},{5,18},{6,17},{7,16},{8,31},{9,... | collective-permute-start | bytes 208904 | tf_op jit(solution)/shard_map/ppermute | solution.py:384
  10.8 7.8 %collective-permute-start.6 = (f32[136,128]{1,0:T(8,128)S(1)}, f32[136,128]{1,0:T(8,128)S(1)}, u32[]{:S(2)}, u32[]{:S(2)}) collective-permute-start(f32[136,128]{1,0:T(8,128)S(1)} %get-tuple-element.51), channel_id=1, source_target_pairs={{0,31},{1,30},{2,29},{3,28},{4,27},{5,26},{6,25},{7,24},{8,23},{9,... | collective-permute-start | bytes 208904 | tf_op jit(solution)/shard_map/ppermute | solution.py:384
  10.9 28.5 %collective-permute-start.1 = (f32[256,128]{1,0:T(8,128)S(1)}, f32[256,128]{1,0:T(8,128)S(1)}, u32[]{:S(2)}, u32[]{:S(2)}) collective-permute-start(f32[256,128]{1,0:T(8,128)S(1)} %get-tuple-element.45), channel_id=1, source_target_pairs={{0,6},{1,7},{2,4},{3,5},{4,2},{5,3},{6,0},{7,1},{8,14},{9,15},{10,... | collective-permute-start | bytes 393224 | tf_op jit(solution)/shard_map/ppermute | solution.py:384
  14.4 28.6 %collective-permute-start.2 = (f32[256,128]{1,0:T(8,128)S(1)}, f32[256,128]{1,0:T(8,128)S(1)}, u32[]{:S(2)}, u32[]{:S(2)}) collective-permute-start(f32[256,128]{1,0:T(8,128)S(1)} %get-tuple-element.46), channel_id=1, source_target_pairs={{0,20},{1,21},{2,22},{3,23},{4,16},{5,17},{6,18},{7,19},{8,28},{9,... | collective-permute-start | bytes 393224 | tf_op jit(solution)/shard_map/ppermute | solution.py:384
  14.4 30.4 %collective-permute-start.3 = (f32[256,128]{1,0:T(8,128)S(1)}, f32[256,128]{1,0:T(8,128)S(1)}, u32[]{:S(2)}, u32[]{:S(2)}) collective-permute-start(f32[256,128]{1,0:T(8,128)S(1)} %get-tuple-element.47), channel_id=1, source_target_pairs={{0,7},{1,6},{2,5},{3,4},{4,3},{5,2},{6,1},{7,0},{8,15},{9,14},{10,... | collective-permute-start | bytes 393224 | tf_op jit(solution)/shard_map/ppermute | solution.py:384
  16.4 22.4 %collective-permute-start.14 = (f32[128,128]{1,0:T(8,128)S(1)}, f32[128,128]{1,0:T(8,128)S(1)}, u32[]{:S(2)}, u32[]{:S(2)}) collective-permute-start(f32[128,128]{1,0:T(8,128)S(1)} %get-tuple-element.66), channel_id=1, source_target_pairs={{0,4},{1,5},{2,6},{3,7},{4,0},{5,1},{6,2},{7,3},{8,12},{9,13},{10,... | collective-permute-start | bytes 196616 | tf_op jit(solution)/shard_map/ppermute | solution.py:384
  18.6 20.7 %collective-permute-start.15 = (f32[128,128]{1,0:T(8,128)S(1)}, f32[128,128]{1,0:T(8,128)S(1)}, u32[]{:S(2)}, u32[]{:S(2)}) collective-permute-start(f32[128,128]{1,0:T(8,128)S(1)} %get-tuple-element.67), channel_id=1, source_target_pairs={{0,12},{1,13},{2,14},{3,15},{4,8},{5,9},{6,10},{7,11},{8,4},{9,5},... | collective-permute-start | bytes 196616 | tf_op jit(solution)/shard_map/ppermute | solution.py:384
  18.8 49.3 %copy-start = (bf16[128,256]{1,0:T(8,128)(2,1)S(1)}, bf16[128,256]{1,0:T(8,128)(2,1)}, u32[]{:S(2)}) copy-start(bf16[128,256]{1,0:T(8,128)(2,1)} %constant.8.clone.refs_0_) | copy-start | bytes 196612
  38.8 12.4 %collective-permute-start.7 = (f32[264,128]{1,0:T(8,128)S(1)}, f32[264,128]{1,0:T(8,128)S(1)}, u32[]{:S(2)}, u32[]{:S(2)}) collective-permute-start(f32[264,128]{1,0:T(8,128)S(1)} %get-tuple-element.59), channel_id=1, source_target_pairs={{0,1},{1,0},{2,3},{3,2},{4,5},{5,4},{6,7},{7,6},{8,9},{9,8},{10,11... | collective-permute-start | bytes 405512 | tf_op jit(solution)/shard_map/ppermute | solution.py:384
  39.3 14.1 %collective-permute-start.8 = (f32[264,128]{1,0:T(8,128)S(1)}, f32[264,128]{1,0:T(8,128)S(1)}, u32[]{:S(2)}, u32[]{:S(2)}) collective-permute-start(f32[264,128]{1,0:T(8,128)S(1)} %get-tuple-element.60), channel_id=1, source_target_pairs={{0,2},{1,3},{2,0},{3,1},{4,6},{5,7},{6,4},{7,5},{8,10},{9,11},{10,... | collective-permute-start | bytes 405512 | tf_op jit(solution)/shard_map/ppermute | solution.py:384
  39.3 11.2 %collective-permute-start.4 = (f32[256,128]{1,0:T(8,128)S(1)}, f32[256,128]{1,0:T(8,128)S(1)}, u32[]{:S(2)}, u32[]{:S(2)}) collective-permute-start(f32[256,128]{1,0:T(8,128)S(1)} %get-tuple-element.48), channel_id=1, source_target_pairs={{0,21},{1,20},{2,23},{3,22},{4,17},{5,16},{6,19},{7,18},{8,29},{9,... | collective-permute-start | bytes 393224 | tf_op jit(solution)/shard_map/ppermute | solution.py:384
  43.0 11.9 %collective-permute-start.9 = (f32[264,128]{1,0:T(8,128)S(1)}, f32[264,128]{1,0:T(8,128)S(1)}, u32[]{:S(2)}, u32[]{:S(2)}) collective-permute-start(f32[264,128]{1,0:T(8,128)S(1)} %get-tuple-element.61), channel_id=1, source_target_pairs={{0,16},{1,17},{2,18},{3,19},{4,20},{5,21},{6,22},{7,23},{8,24},{9,... | collective-permute-start | bytes 405512 | tf_op jit(solution)/shard_map/ppermute | solution.py:384
  44.8 12.1 %collective-permute-start.10 = (f32[264,128]{1,0:T(8,128)S(1)}, f32[264,128]{1,0:T(8,128)S(1)}, u32[]{:S(2)}, u32[]{:S(2)}) collective-permute-start(f32[264,128]{1,0:T(8,128)S(1)} %get-tuple-element.62), channel_id=1, source_target_pairs={{0,3},{1,2},{2,1},{3,0},{4,7},{5,6},{6,5},{7,4},{8,11},{9,10},{10,... | collective-permute-start | bytes 405512 | tf_op jit(solution)/shard_map/ppermute | solution.py:384
  50.6 11.4 %collective-permute-start.11 = (f32[264,128]{1,0:T(8,128)S(1)}, f32[264,128]{1,0:T(8,128)S(1)}, u32[]{:S(2)}, u32[]{:S(2)}) collective-permute-start(f32[264,128]{1,0:T(8,128)S(1)} %get-tuple-element.63), channel_id=1, source_target_pairs={{0,17},{1,16},{2,19},{3,18},{4,21},{5,20},{6,23},{7,22},{8,25},{9,... | collective-permute-start | bytes 405512 | tf_op jit(solution)/shard_map/ppermute | solution.py:384
  51.2 10.7 %collective-permute-start.12 = (f32[264,128]{1,0:T(8,128)S(1)}, f32[264,128]{1,0:T(8,128)S(1)}, u32[]{:S(2)}, u32[]{:S(2)}) collective-permute-start(f32[264,128]{1,0:T(8,128)S(1)} %get-tuple-element.64), channel_id=1, source_target_pairs={{0,18},{1,19},{2,16},{3,17},{4,22},{5,23},{6,20},{7,21},{8,26},{9,... | collective-permute-start | bytes 405512 | tf_op jit(solution)/shard_map/ppermute | solution.py:384
  53.4 8.6 %collective-permute-start.13 = (f32[264,128]{1,0:T(8,128)S(1)}, f32[264,128]{1,0:T(8,128)S(1)}, u32[]{:S(2)}, u32[]{:S(2)}) collective-permute-start(f32[264,128]{1,0:T(8,128)S(1)} %get-tuple-element.65), channel_id=1, source_target_pairs={{0,19},{1,18},{2,17},{3,16},{4,23},{5,22},{6,21},{7,20},{8,27},{9,... | collective-permute-start | bytes 405512 | tf_op jit(solution)/shard_map/ppermute | solution.py:384
  54.9 13.2 %collective-permute-start.16 = (f32[256,128]{1,0:T(8,128)S(1)}, f32[256,128]{1,0:T(8,128)S(1)}, u32[]{:S(2)}, u32[]{:S(2)}) collective-permute-start(f32[256,128]{1,0:T(8,128)S(1)} %get-tuple-element.70), channel_id=1, source_target_pairs={{0,5},{1,4},{2,7},{3,6},{4,1},{5,0},{6,3},{7,2},{8,13},{9,12},{10,... | collective-permute-start | bytes 393224 | tf_op jit(solution)/shard_map/ppermute | solution.py:384
  56.9 11.3 %collective-permute-start.17 = (f32[256,128]{1,0:T(8,128)S(1)}, f32[256,128]{1,0:T(8,128)S(1)}, u32[]{:S(2)}, u32[]{:S(2)}) collective-permute-start(f32[256,128]{1,0:T(8,128)S(1)} %get-tuple-element.71), channel_id=1, source_target_pairs={{0,22},{1,23},{2,20},{3,21},{4,18},{5,19},{6,16},{7,17},{8,30},{9,... | collective-permute-start | bytes 393224 | tf_op jit(solution)/shard_map/ppermute | solution.py:384
where the time goes:
time: 70.5 us; the launch traced here: 70.3 us
  waiting for transfers between devices  34.2 us (49%)
  starting transfers between devices  30 us (43%)
  Pallas kernels  5.43 us (8%)
    ppermute x18, waiting for transfers between devices, exchange(): return lax.ppermute(values, AXES, pairs_of)  34.2 us
    ppermute x18, starting transfers between devices, exchange(): return lax.ppermute(values, AXES, pairs_of)  30 us
    pallas_call x1, Pallas kernels, per_device(): pl.pallas_call(lambda *refs: transform_kernel(info, targets, tiles, *refs...  3.06 us
    pallas_call x1, Pallas kernels, per_device(): pl.pallas_call(lambda *refs: place_kernel(place_info, late_sources, *refs...  2.17 us
  transfers between devices with their start and end apart: 18, of which 5 were waited for; matrix products, arithmetic and copies ran while one was open for 0% of the time, Pallas kernels for 0%

commit v1 on v0

--- a/solution.py
+++ b/solution.py
@@ -255,12 +255,11 @@
                 turned = dot_rows(order, jnp.concatenate([high, low], 1))
                 row = (group * RADIX + residue) * 2 * LANES + part
                 out_ref[pl.ds(row, LANES, stride=2), :] = turned * factor
-            if residue % 2 == 1:
-                size = 4 * LANES
-                span = pl.ds(len(copies) * size, size)
-                sem = sems.at[len(copies)]
-                copies.append(pltpu.make_async_copy(out_ref.at[span], out_hbm.at[span], sem))
-                copies[-1].start()
+            size = 2 * LANES
+            span = pl.ds(len(copies) * size, size)
+            sem = sems.at[len(copies)]
+            copies.append(pltpu.make_async_copy(out_ref.at[span], out_hbm.at[span], sem))
+            copies[-1].start()
     for copy in copies:
         copy.wait()
 
@@ -473,7 +472,7 @@
         input_output_aliases={1: 2},
         scratch_shapes=[
             pltpu.VMEM((vectors, LANES), jnp.float32),
-            pltpu.SemaphoreType.DMA((2 * groups,)),
+            pltpu.SemaphoreType.DMA((RADIX * groups,)),
         ],
         compiler_params=params,
         name="place",

time: 70.5 us -> 70.5 us (level)
  no operation moved by 1% of the time
where the time goes in v1:
time: 70.5 us; the launch traced here: 70.3 us
  waiting for transfers between devices  34.2 us (49%)
  starting transfers between devices  30 us (43%)
  Pallas kernels  5.46 us (8%)
    ppermute x18, waiting for transfers between devices, exchange(): return lax.ppermute(values, AXES, pairs_of)  34.2 us
    ppermute x18, starting transfers between devices, exchange(): return lax.ppermute(values, AXES, pairs_of)  30 us
    pallas_call x1, Pallas kernels, per_device(): pl.pallas_call(lambda *refs: transform_kernel(info, targets, tiles, *refs...  3.06 us
    pallas_call x1, Pallas kernels, per_device(): pl.pallas_call(lambda *refs: place_kernel(place_info, late_sources, *refs...  2.19 us
  transfers between devices with their start and end apart: 18, of which 5 were waited for; matrix products, arithmetic and copies ran while one was open for 0% of the time, Pallas kernels for 0%

profile of v1, /device:TPU:0, one launch (start us, length us, event | category | flops | bytes accessed | tf_op | source)
XLA Modules:
  0.0 70.3 jit_solution(5061395281830712134)
XLA Ops:
  0.6 3.1 %transform.1 = (f32[256,128]{1,0:T(8,128)S(1)}, f32[256,128]{1,0:T(8,128)S(1)}, f32[256,128]{1,0:T(8,128)S(1)}, f32[256,128]{1,0:T(8,128)S(1)}, f32[256,128]{1,0...) custom-call(f32[4096,128]{1,0:T(8,128)} %bitcast.10, ...), custom_call_target="tpu_custom_call" | custom-call | tf_op jit(solution)/shard_map/transform/pallas_call | solution.py:399
  3.7 0.6 collective-permute-start
  4.2 6.5 %collective-permute-start.5 = (f32[136,128]{1,0:T(8,128)S(1)}, f32[136,128]{1,0:T(8,128)S(1)}, u32[]{:S(2)}, u32[]{:S(2)}) collective-permute-start(f32[136,128]{1,0:T(8,128)S(1)} %get-tuple-element.50), channel_id=1, source_target_pairs={{0,23},{1,22},{2,21},{3,20},{4,19},{5,18},{6,17},{7,16},{8,31},{9,... | collective-permute-start | bytes 208904 | tf_op jit(solution)/shard_map/ppermute | solution.py:383
  10.8 0.0 collective-permute-start.6
  10.8 0.0 collective-permute-done.refs_0_.refs_12_
  10.9 3.5 %collective-permute-start.1 = (f32[256,128]{1,0:T(8,128)S(1)}, f32[256,128]{1,0:T(8,128)S(1)}, u32[]{:S(2)}, u32[]{:S(2)}) collective-permute-start(f32[256,128]{1,0:T(8,128)S(1)} %get-tuple-element.45), channel_id=1, source_target_pairs={{0,6},{1,7},{2,4},{3,5},{4,2},{5,3},{6,0},{7,1},{8,14},{9,15},{10,... | collective-permute-start | bytes 393224 | tf_op jit(solution)/shard_map/ppermute | solution.py:383
  14.4 2.0 %collective-permute-start.3 = (f32[256,128]{1,0:T(8,128)S(1)}, f32[256,128]{1,0:T(8,128)S(1)}, u32[]{:S(2)}, u32[]{:S(2)}) collective-permute-start(f32[256,128]{1,0:T(8,128)S(1)} %get-tuple-element.47), channel_id=1, source_target_pairs={{0,7},{1,6},{2,5},{3,4},{4,3},{5,2},{6,1},{7,0},{8,15},{9,14},{10,... | collective-permute-start | bytes 393224 | tf_op jit(solution)/shard_map/ppermute | solution.py:383
  16.4 2.1 %collective-permute-start.14 = (f32[128,128]{1,0:T(8,128)S(1)}, f32[128,128]{1,0:T(8,128)S(1)}, u32[]{:S(2)}, u32[]{:S(2)}) collective-permute-start(f32[128,128]{1,0:T(8,128)S(1)} %get-tuple-element.66), channel_id=1, source_target_pairs={{0,4},{1,5},{2,6},{3,7},{4,0},{5,1},{6,2},{7,3},{8,12},{9,13},{10,... | collective-permute-start | bytes 196616 | tf_op jit(solution)/shard_map/ppermute | solution.py:383
  18.5 0.1 collective-permute-done.6.refs_3_.refs_14_
  18.6 0.2 collective-permute-start.15
  18.8 20.0 %collective-permute-done.14.refs_15_ = f32[128,128]{1,0:T(8,128)S(1)} collective-permute-done((f32[128,128]{1,0:T(8,128)S(1)}, f32[128,128]{1,0:T(8,128)S(1)}, u32[]{:S(2)}, u32[]{:S(2)}) %collective-permute-start.14) | collective-permute-done | bytes 65568 | tf_op jit(solution)/shard_map/ppermute | solution.py:383
  38.8 0.5 collective-permute-start.7
  39.3 3.7 %collective-permute-start.4 = (f32[256,128]{1,0:T(8,128)S(1)}, f32[256,128]{1,0:T(8,128)S(1)}, u32[]{:S(2)}, u32[]{:S(2)}) collective-permute-start(f32[256,128]{1,0:T(8,128)S(1)} %get-tuple-element.48), channel_id=1, source_target_pairs={{0,21},{1,20},{2,23},{3,22},{4,17},{5,16},{6,19},{7,18},{8,29},{9,... | collective-permute-start | bytes 393224 | tf_op jit(solution)/shard_map/ppermute | solution.py:383
  43.0 1.8 %collective-permute-start.9 = (f32[264,128]{1,0:T(8,128)S(1)}, f32[264,128]{1,0:T(8,128)S(1)}, u32[]{:S(2)}, u32[]{:S(2)}) collective-permute-start(f32[264,128]{1,0:T(8,128)S(1)} %get-tuple-element.61), channel_id=1, source_target_pairs={{0,16},{1,17},{2,18},{3,19},{4,20},{5,21},{6,22},{7,23},{8,24},{9,... | collective-permute-start | bytes 405512 | tf_op jit(solution)/shard_map/ppermute | solution.py:383
  44.8 5.8 %collective-permute-done.4.refs_3_ = f32[256,128]{1,0:T(8,128)S(1)} collective-permute-done((f32[256,128]{1,0:T(8,128)S(1)}, f32[256,128]{1,0:T(8,128)S(1)}, u32[]{:S(2)}, u32[]{:S(2)}) %collective-permute-start.4) | collective-permute-done | bytes 131104 | tf_op jit(solution)/shard_map/ppermute | solution.py:383
  50.6 0.7 collective-permute-start.11
  51.2 2.2 %collective-permute-start.12 = (f32[264,128]{1,0:T(8,128)S(1)}, f32[264,128]{1,0:T(8,128)S(1)}, u32[]{:S(2)}, u32[]{:S(2)}) collective-permute-start(f32[264,128]{1,0:T(8,128)S(1)} %get-tuple-element.64), channel_id=1, source_target_pairs={{0,18},{1,19},{2,16},{3,17},{4,22},{5,23},{6,20},{7,21},{8,26},{9,... | collective-permute-start | bytes 405512 | tf_op jit(solution)/shard_map/ppermute | solution.py:383
  53.4 1.5 %collective-permute-start.13 = (f32[264,128]{1,0:T(8,128)S(1)}, f32[264,128]{1,0:T(8,128)S(1)}, u32[]{:S(2)}, u32[]{:S(2)}) collective-permute-start(f32[264,128]{1,0:T(8,128)S(1)} %get-tuple-element.65), channel_id=1, source_target_pairs={{0,19},{1,18},{2,17},{3,16},{4,23},{5,22},{6,21},{7,20},{8,27},{9,... | collective-permute-start | bytes 405512 | tf_op jit(solution)/shard_map/ppermute | solution.py:383
  54.9 2.0 %collective-permute-start.16 = (f32[256,128]{1,0:T(8,128)S(1)}, f32[256,128]{1,0:T(8,128)S(1)}, u32[]{:S(2)}, u32[]{:S(2)}) collective-permute-start(f32[256,128]{1,0:T(8,128)S(1)} %get-tuple-element.70), channel_id=1, source_target_pairs={{0,5},{1,4},{2,7},{3,6},{4,1},{5,0},{6,3},{7,2},{8,13},{9,12},{10,... | collective-permute-start | bytes 393224 | tf_op jit(solution)/shard_map/ppermute | solution.py:383
  56.9 2.7 %collective-permute-start.17 = (f32[256,128]{1,0:T(8,128)S(1)}, f32[256,128]{1,0:T(8,128)S(1)}, u32[]{:S(2)}, u32[]{:S(2)}) collective-permute-start(f32[256,128]{1,0:T(8,128)S(1)} %get-tuple-element.71), channel_id=1, source_target_pairs={{0,22},{1,23},{2,20},{3,21},{4,18},{5,19},{6,16},{7,17},{8,30},{9,... | collective-permute-start | bytes 393224 | tf_op jit(solution)/shard_map/ppermute | solution.py:383
  59.6 2.4 %collective-permute-done.11.refs_8_ = f32[264,128]{1,0:T(8,128)S(1)} collective-permute-done((f32[264,128]{1,0:T(8,128)S(1)}, f32[264,128]{1,0:T(8,128)S(1)}, u32[]{:S(2)}, u32[]{:S(2)}) %collective-permute-start.11) | collective-permute-done | bytes 135200 | tf_op jit(solution)/shard_map/ppermute | solution.py:383
  62.0 0.1 stash.1
  62.1 6.0 %collective-permute-done.16.refs_3_ = f32[256,128]{1,0:T(8,128)S(1)} collective-permute-done((f32[256,128]{1,0:T(8,128)S(1)}, f32[256,128]{1,0:T(8,128)S(1)}, u32[]{:S(2)}, u32[]{:S(2)}) %collective-permute-start.16) | collective-permute-done | bytes 131104 | tf_op jit(solution)/shard_map/ppermute | solution.py:383
  68.1 2.2 %place.1 = (f32[4096,128]{1,0:T(8,128)}, f32[3]{0:T(128)}, f32[4352,128]{1,0:T(8,128)S(1)}) custom-call(bf16[128,256]{1,0:T(8,128)(2,1)S(1)} %copy-done, f32[4352,128]{1,0:T(8,128)S(1)} %get-tuple-element.68.refs_1_, f32[8,128]{1,0:T(8,128)S(1)} %get-tuple-element.69.refs_2_, ...), custom_call_target="tpu_custom_call", output_to_operand_aliasing={{2}: (1, {})} | custom-call | tf_op jit(solution)/shard_map/place/pallas_call | solution.py:463
  (19 shorter events, 0.1 us)
Async XLA Ops:
  3.7 7.1 %collective-permute-start = (f32[1800,128]{1,0:T(8,128)S(1)}, f32[1800,128]{1,0:T(8,128)S(1)}, u32[]{:S(2)}, u32[]{:S(2)}) collective-permute-start(f32[1800,128]{1,0:T(8,128)S(1)} %get-tuple-element.38), channel_id=1, source_target_pairs={{0,8},{1,9},{2,10},{3,11},{4,12},{5,13},{6,14},{7,15},{8,0},{9,1},... | collective-permute-start | bytes 2764808 | tf_op jit(solution)/shard_map/ppermute | solution.py:383
  4.2 12.1 %collective-permute-start.5 = (f32[136,128]{1,0:T(8,128)S(1)}, f32[136,128]{1,0:T(8,128)S(1)}, u32[]{:S(2)}, u32[]{:S(2)}) collective-permute-start(f32[136,128]{1,0:T(8,128)S(1)} %get-tuple-element.50), channel_id=1, source_target_pairs={{0,23},{1,22},{2,21},{3,20},{4,19},{5,18},{6,17},{7,16},{8,31},{9,... | collective-permute-start | bytes 208904 | tf_op jit(solution)/shard_map/ppermute | solution.py:383
  10.8 7.8 %collective-permute-start.6 = (f32[136,128]{1,0:T(8,128)S(1)}, f32[136,128]{1,0:T(8,128)S(1)}, u32[]{:S(2)}, u32[]{:S(2)}) collective-permute-start(f32[136,128]{1,0:T(8,128)S(1)} %get-tuple-element.51), channel_id=1, source_target_pairs={{0,31},{1,30},{2,29},{3,28},{4,27},{5,26},{6,25},{7,24},{8,23},{9,... | collective-permute-start | bytes 208904 | tf_op jit(solution)/shard_map/ppermute | solution.py:383
  10.9 28.5 %collective-permute-start.1 = (f32[256,128]{1,0:T(8,128)S(1)}, f32[256,128]{1,0:T(8,128)S(1)}, u32[]{:S(2)}, u32[]{:S(2)}) collective-permute-start(f32[256,128]{1,0:T(8,128)S(1)} %get-tuple-element.45), channel_id=1, source_target_pairs={{0,6},{1,7},{2,4},{3,5},{4,2},{5,3},{6,0},{7,1},{8,14},{9,15},{10,... | collective-permute-start | bytes 393224 | tf_op jit(solution)/shard_map/ppermute | solution.py:383
  14.4 28.6 %collective-permute-start.2 = (f32[256,128]{1,0:T(8,128)S(1)}, f32[256,128]{1,0:T(8,128)S(1)}, u32[]{:S(2)}, u32[]{:S(2)}) collective-permute-start(f32[256,128]{1,0:T(8,128)S(1)} %get-tuple-element.46), channel_id=1, source_target_pairs={{0,20},{1,21},{2,22},{3,23},{4,16},{5,17},{6,18},{7,19},{8,28},{9,... | collective-permute-start | bytes 393224 | tf_op jit(solution)/shard_map/ppermute | solution.py:383
  14.4 30.4 %collective-permute-start.3 = (f32[256,128]{1,0:T(8,128)S(1)}, f32[256,128]{1,0:T(8,128)S(1)}, u32[]{:S(2)}, u32[]{:S(2)}) collective-permute-start(f32[256,128]{1,0:T(8,128)S(1)} %get-tuple-element.47), channel_id=1, source_target_pairs={{0,7},{1,6},{2,5},{3,4},{4,3},{5,2},{6,1},{7,0},{8,15},{9,14},{10,... | collective-permute-start | bytes 393224 | tf_op jit(solution)/shard_map/ppermute | solution.py:383
  16.4 22.4 %collective-permute-start.14 = (f32[128,128]{1,0:T(8,128)S(1)}, f32[128,128]{1,0:T(8,128)S(1)}, u32[]{:S(2)}, u32[]{:S(2)}) collective-permute-start(f32[128,128]{1,0:T(8,128)S(1)} %get-tuple-element.66), channel_id=1, source_target_pairs={{0,4},{1,5},{2,6},{3,7},{4,0},{5,1},{6,2},{7,3},{8,12},{9,13},{10,... | collective-permute-start | bytes 196616 | tf_op jit(solution)/shard_map/ppermute | solution.py:383
  18.6 20.7 %collective-permute-start.15 = (f32[128,128]{1,0:T(8,128)S(1)}, f32[128,128]{1,0:T(8,128)S(1)}, u32[]{:S(2)}, u32[]{:S(2)}) collective-permute-start(f32[128,128]{1,0:T(8,128)S(1)} %get-tuple-element.67), channel_id=1, source_target_pairs={{0,12},{1,13},{2,14},{3,15},{4,8},{5,9},{6,10},{7,11},{8,4},{9,5},... | collective-permute-start | bytes 196616 | tf_op jit(solution)/shard_map/ppermute | solution.py:383
  18.8 49.3 %copy-start = (bf16[128,256]{1,0:T(8,128)(2,1)S(1)}, bf16[128,256]{1,0:T(8,128)(2,1)}, u32[]{:S(2)}) copy-start(bf16[128,256]{1,0:T(8,128)(2,1)} %constant.8.clone.refs_0_) | copy-start | bytes 196612
  38.8 12.4 %collective-permute-start.7 = (f32[264,128]{1,0:T(8,128)S(1)}, f32[264,128]{1,0:T(8,128)S(1)}, u32[]{:S(2)}, u32[]{:S(2)}) collective-permute-start(f32[264,128]{1,0:T(8,128)S(1)} %get-tuple-element.59), channel_id=1, source_target_pairs={{0,1},{1,0},{2,3},{3,2},{4,5},{5,4},{6,7},{7,6},{8,9},{9,8},{10,11... | collective-permute-start | bytes 405512 | tf_op jit(solution)/shard_map/ppermute | solution.py:383
  39.3 14.1 %collective-permute-start.8 = (f32[264,128]{1,0:T(8,128)S(1)}, f32[264,128]{1,0:T(8,128)S(1)}, u32[]{:S(2)}, u32[]{:S(2)}) collective-permute-start(f32[264,128]{1,0:T(8,128)S(1)} %get-tuple-element.60), channel_id=1, source_target_pairs={{0,2},{1,3},{2,0},{3,1},{4,6},{5,7},{6,4},{7,5},{8,10},{9,11},{10,... | collective-permute-start | bytes 405512 | tf_op jit(solution)/shard_map/ppermute | solution.py:383
  39.3 11.2 %collective-permute-start.4 = (f32[256,128]{1,0:T(8,128)S(1)}, f32[256,128]{1,0:T(8,128)S(1)}, u32[]{:S(2)}, u32[]{:S(2)}) collective-permute-start(f32[256,128]{1,0:T(8,128)S(1)} %get-tuple-element.48), channel_id=1, source_target_pairs={{0,21},{1,20},{2,23},{3,22},{4,17},{5,16},{6,19},{7,18},{8,29},{9,... | collective-permute-start | bytes 393224 | tf_op jit(solution)/shard_map/ppermute | solution.py:383
  43.0 11.9 %collective-permute-start.9 = (f32[264,128]{1,0:T(8,128)S(1)}, f32[264,128]{1,0:T(8,128)S(1)}, u32[]{:S(2)}, u32[]{:S(2)}) collective-permute-start(f32[264,128]{1,0:T(8,128)S(1)} %get-tuple-element.61), channel_id=1, source_target_pairs={{0,16},{1,17},{2,18},{3,19},{4,20},{5,21},{6,22},{7,23},{8,24},{9,... | collective-permute-start | bytes 405512 | tf_op jit(solution)/shard_map/ppermute | solution.py:383
  44.8 12.1 %collective-permute-start.10 = (f32[264,128]{1,0:T(8,128)S(1)}, f32[264,128]{1,0:T(8,128)S(1)}, u32[]{:S(2)}, u32[]{:S(2)}) collective-permute-start(f32[264,128]{1,0:T(8,128)S(1)} %get-tuple-element.62), channel_id=1, source_target_pairs={{0,3},{1,2},{2,1},{3,0},{4,7},{5,6},{6,5},{7,4},{8,11},{9,10},{10,... | collective-permute-start | bytes 405512 | tf_op jit(solution)/shard_map/ppermute | solution.py:383
  50.6 11.4 %collective-permute-start.11 = (f32[264,128]{1,0:T(8,128)S(1)}, f32[264,128]{1,0:T(8,128)S(1)}, u32[]{:S(2)}, u32[]{:S(2)}) collective-permute-start(f32[264,128]{1,0:T(8,128)S(1)} %get-tuple-element.63), channel_id=1, source_target_pairs={{0,17},{1,16},{2,19},{3,18},{4,21},{5,20},{6,23},{7,22},{8,25},{9,... | collective-permute-start | bytes 405512 | tf_op jit(solution)/shard_map/ppermute | solution.py:383
  51.2 10.7 %collective-permute-start.12 = (f32[264,128]{1,0:T(8,128)S(1)}, f32[264,128]{1,0:T(8,128)S(1)}, u32[]{:S(2)}, u32[]{:S(2)}) collective-permute-start(f32[264,128]{1,0:T(8,128)S(1)} %get-tuple-element.64), channel_id=1, source_target_pairs={{0,18},{1,19},{2,16},{3,17},{4,22},{5,23},{6,20},{7,21},{8,26},{9,... | collective-permute-start | bytes 405512 | tf_op jit(solution)/shard_map/ppermute | solution.py:383
  53.4 8.6 %collective-permute-start.13 = (f32[264,128]{1,0:T(8,128)S(1)}, f32[264,128]{1,0:T(8,128)S(1)}, u32[]{:S(2)}, u32[]{:S(2)}) collective-permute-start(f32[264,128]{1,0:T(8,128)S(1)} %get-tuple-element.65), channel_id=1, source_target_pairs={{0,19},{1,18},{2,17},{3,16},{4,23},{5,22},{6,21},{7,20},{8,27},{9,... | collective-permute-start | bytes 405512 | tf_op jit(solution)/shard_map/ppermute | solution.py:383
  54.9 13.2 %collective-permute-start.16 = (f32[256,128]{1,0:T(8,128)S(1)}, f32[256,128]{1,0:T(8,128)S(1)}, u32[]{:S(2)}, u32[]{:S(2)}) collective-permute-start(f32[256,128]{1,0:T(8,128)S(1)} %get-tuple-element.70), channel_id=1, source_target_pairs={{0,5},{1,4},{2,7},{3,6},{4,1},{5,0},{6,3},{7,2},{8,13},{9,12},{10,... | collective-permute-start | bytes 393224 | tf_op jit(solution)/shard_map/ppermute | solution.py:383
  56.9 11.3 %collective-permute-start.17 = (f32[256,128]{1,0:T(8,128)S(1)}, f32[256,128]{1,0:T(8,128)S(1)}, u32[]{:S(2)}, u32[]{:S(2)}) collective-permute-start(f32[256,128]{1,0:T(8,128)S(1)} %get-tuple-element.71), channel_id=1, source_target_pairs={{0,22},{1,23},{2,20},{3,21},{4,18},{5,19},{6,16},{7,17},{8,30},{9,... | collective-permute-start | bytes 393224 | tf_op jit(solution)/shard_map/ppermute | solution.py:383
